TPU v7x, 32 devices: a whole 2x2x4 slice. The times are simulated.
32 devices in a mesh: parts: 1, var: 8 (over z, core), patch: 4 (over y, x).
Axes of the slice: x: 2, y: 2, z: 4, core: 2. Of those that a mesh axis runs over, the one named last changes fastest.
Arguments:
- tokens: bfloat16 [256, 24, 768], P('patch', ('parts', 'var')), may hold values from -6 to 6
- patch_mask: int32 [256, 24], P('patch', ('parts', 'var')), may hold values 0 or 1
- group_ids: int32 [24], P('parts'), may hold values from 0 to 7, never falling along the last dimension, each value on 1 to 6 neighbouring positions
- time_gain: float32 [768], replicated, may hold values from 0.1 to 1.9
- time_qkv: bfloat16 [768, 3, 768], P(None, None, 'patch'), may hold values from -0.21875 to 0.21875
- time_out: bfloat16 [768, 768], P('patch'), may hold values from -0.21875 to 0.21875
- space_gain: float32 [768], replicated, may hold values from 0.1 to 1.9
- space_qkv: bfloat16 [768, 3, 768], P(None, None, 'patch'), may hold values from -0.21875 to 0.21875
- space_out: bfloat16 [768, 768], P('patch'), may hold values from -0.21875 to 0.21875
Outputs:
- panel_out: bfloat16 [256, 24, 768], P('patch', ('parts', 'var'))
Inputs may be any that keep to these rules, and one draw needn't show every extreme that they name: group_ids never falls along the variates; each group is a run of 1 to 6 consecutive variates.
All inputs are finite; a program needn't handle non-finite values. No bound on the sum of `patch_mask` on one device may be relied on, other than what follows from the above.
Results may differ from a plain program's by a relative error of at most 0.017.
Values may be sent and summed in bfloat16 or wider, within the bound.
A program may use at most 64 MiB of HBM per device.

v0:
```python
import functools

import jax
import jax.numpy as jnp
from jax import lax
from jax.experimental import pallas as pl
from jax.experimental.pallas import tpu as pltpu
from jax.sharding import PartitionSpec as P

HD = 64
REACH = 5
EPS = 1e-06
MESH = pl.DeviceIdType.MESH
F32 = jnp.float32
BF16 = jnp.bfloat16


def norm_rows(rows, gain):
    floats = rows.astype(F32)
    scaled = floats * lax.rsqrt(jnp.mean(floats * floats, axis=-1, keepdims=True) + EPS)
    return (scaled * gain).astype(BF16)


def dot(a, b):
    return jnp.dot(a, b, preferred_element_type=F32)


def dot_t(a, b):
    return lax.dot_general(a, b, (((1,), (1,)), ((), ())), preferred_element_type=F32)


def kernel(
    n, nvar, tok, marks, gids, tgain, sgain, wt_in, wot_in, wqs_in, wos_in,
    out, gx, mk, wt, wot, wqs, wos, att, ratt, mid, sw, kvb, qb, prod, sc, pb,
    local_sem, tok_s, tok_r, mk_s, mk_r, w_s, w_r, att_s, att_r, win_s, win_r,
):
    me = lax.axis_index("patch")
    var = lax.axis_index("var")
    nv, pp, dm = tok.shape
    hw = wot_in.shape[0]
    heads = hw // HD
    side = (me + 1 - 2 * (me % 2), me + 2 - 4 * ((me // 2) % 2), n - 1 - me)
    sib = var + 1 - 2 * (var % 2)
    core = var % 2
    nbrs = (1, -1, 2, -2)

    def exists(k):
        return (var + k >= 0) & (var + k < nvar)

    barrier = pltpu.get_barrier_semaphore()
    count = n - 1 + 1
    for other in side:
        pl.semaphore_signal(barrier, inc=1, device_id={"patch": other}, device_id_type=MESH)
    pl.semaphore_signal(barrier, inc=1, device_id={"var": sib}, device_id_type=MESH)
    for k in nbrs:
        @pl.when(exists(k))
        def _():
            pl.semaphore_signal(barrier, inc=1, device_id={"var": var + k}, device_id_type=MESH)
        count = count + exists(k).astype(jnp.int32)
    own = [
        pltpu.make_async_copy(wot_in, wot.at[me], local_sem.at[0]),
        pltpu.make_async_copy(wqs_in, wqs.at[me], local_sem.at[1]),
        pltpu.make_async_copy(wos_in, wos.at[me], local_sem.at[2]),
        pltpu.make_async_copy(wt_in, wt, local_sem.at[3]),
        pltpu.make_async_copy(tok, gx.at[:, pl.ds(pl.multiple_of(me * pp, pp), pp), :], local_sem.at[4]),
    ]
    for i in (4, 3, 0, 1, 2):
        own[i].start()
    pl.semaphore_wait(barrier, count)

    sends = []

    def remote(src, dst, ssem, rsem, **where):
        c = pltpu.make_async_remote_copy(
            src_ref=src, dst_ref=dst, send_sem=ssem, recv_sem=rsem, device_id=where, device_id_type=MESH
        )
        return c

    def launch(*a, **k):
        c = remote(*a, **k)
        c.start()
        sends.append(c)
        return c

    def block(of, lo=0, num=pp):
        return pl.ds(pl.multiple_of(of * pp + lo, num), num)

    half = pp // 2
    mk_c = [launch(marks, mk.at[me], mk_s.at[d], mk_r.at[d], patch=side[d]) for d in range(3)]
    tok_c = {}
    for i in range(nv):
        for d in (0, 1):
            v = i if d == 1 else nv - 1 - i
            tok_c[d, v] = launch(tok.at[v], gx.at[v, block(me), :], tok_s.at[d, v], tok_r.at[d, v], patch=side[d])
    routes = ((1, 0, 0, pp), (0, 2, 0, pp), (1, 1, 0, half), (0, 1, half, half))
    diag_c = []
    for i, (d, v, lo, num) in enumerate(routes):
        tok_c[d, v].wait_recv()
        piece = gx.at[v, block(side[d], lo, num), :]
        diag_c.append(launch(piece, piece, tok_s.at[2, i], tok_r.at[2, i], patch=side[1 - d]))

    arrays = ((wot_in, wot), (wqs_in, wqs), (wos_in, wos))
    wc = {}

    def piece_of(a, shard, part=None):
        rows = arrays[a][1].shape[1] // 2
        if part is None:
            return arrays[a][1].at[shard, pl.ds(pl.multiple_of(core * rows, rows), rows), :]
        num = rows // 2
        return arrays[a][1].at[shard, pl.ds(pl.multiple_of(core * rows + part * num, num), num), :]

    def w_own(a):
        src = arrays[a][0]
        rows = src.shape[0] // 2
        for d in (0, 1):
            wc[a, d] = launch(
                src.at[pl.ds(pl.multiple_of(core * rows, rows), rows), :], piece_of(a, me),
                w_s.at[a, d], w_r.at[a, d], patch=side[d],
            )

    def w_relay(a):
        for d in (0, 1):
            wc[a, d].wait_recv()
            piece = piece_of(a, side[d], 1 - d)
            wc[a, 2 + d] = launch(piece, piece, w_s.at[a, 2 + d], w_r.at[a, 2 + d], patch=side[1 - d])
            piece = piece_of(a, side[d])
            wc[a, 4 + d] = launch(piece, piece, w_s.at[a, 4 + d], w_r.at[a, 4 + d], var=sib)

    def w_diag(a):
        wc[a, 2].wait_recv()
        wc[a, 3].wait_recv()
        piece = piece_of(a, side[2])
        wc[a, 6] = launch(piece, piece, w_s.at[a, 6], w_r.at[a, 6], var=sib)

    w_own(0)
    w_own(2)
    for k in nbrs:
        lo = {1: 9, -1: 3, 2: 12, -2: 1}[k]
        num = nv if abs(k) == 1 else nv - 1

        @pl.when(jnp.logical_not(exists(k)))
        def _():
            sw[lo:lo + num] = jnp.zeros((num, pp, dm), BF16)

    mk[me] = marks[...]
    own[3].wait()
    own[4].wait()
    for c in mk_c:
        c.wait_recv()
    for d in (0, 1):
        for v in range(nv):
            if (d, v) not in [r[:2] for r in routes]:
                tok_c[d, v].wait_recv()
    for c in diag_c:
        c.wait_recv()

    full = n * pp
    seen = jnp.concatenate([mk[s] for s in range(n)], axis=1)
    qi = lax.broadcasted_iota(jnp.int32, (full, full), 0)
    ki = lax.broadcasted_iota(jnp.int32, (full, full), 1)
    att_c = []
    for v in range(nv):
        normed = norm_rows(gx[v], tgain[...])
        proj = dot_t(normed, wt[...]).astype(BF16)
        allowed = ((ki < qi) & (seen[v:v + 1, :] > 0)) | (ki == qi)
        outs = []
        for h in range(heads):
            q = proj[:, h * HD:(h + 1) * HD]
            k = proj[:, hw + h * HD:hw + (h + 1) * HD]
            val = proj[:, 2 * hw + h * HD:2 * hw + (h + 1) * HD]
            s = lax.dot_general(q, k, (((1,), (1,)), ((), ())), preferred_element_type=F32) * HD ** (-0.5)
            s = jnp.where(allowed, s, -jnp.inf)
            e = jnp.exp(s - jnp.max(s, axis=-1, keepdims=True))
            w = (e / jnp.sum(e, axis=-1, keepdims=True)).astype(BF16)
            outs.append(dot(w, val).astype(BF16))
        att[v] = jnp.concatenate(outs, axis=1)
        for d in (2, 0, 1):
            att_c.append(launch(att.at[v, block(side[d]), :], ratt.at[me, v], att_s.at[v, d], att_r.at[v, d], patch=side[d]))
        ratt[me, v] = att[v, block(me), :]
    w_relay(0)
    w_own(1)
    own[0].wait()
    for c in att_c:
        c.wait_recv()
    w_diag(0)
    for k in (4, 5, 6):
        wc[0, k].wait_recv()

    rows = nv * pp
    mix = jnp.zeros((rows, dm), F32)
    for s in range(n):
        mix = mix + dot(ratt[s].reshape(rows, hw), wot[s]).astype(BF16).astype(F32)
    middle = (gx[:, block(me), :].reshape(rows, dm).astype(F32) + mix).astype(BF16)
    mid[...] = middle
    sw[6:6 + nv] = norm_rows(middle, sgain[...]).reshape(nv, pp, dm)

    def window(k, i):
        src = {1: (6, 9), -1: (6, 9), 2: (7, 9), -2: (6, 8)}[k]
        dst = {1: (3, 6), -1: (9, 12), 2: (1, 3), -2: (12, 14)}[k]
        return remote(sw.at[src[0]:src[1]], sw.at[dst[0]:dst[1]], win_s.at[i], win_r.at[i], var=var + k)

    for i, k in enumerate(nbrs):
        @pl.when(exists(k))
        def _():
            window(k, i).start()

    own[1].wait()
    own[2].wait()
    w_relay(1)
    w_relay(2)
    for i, k in enumerate(nbrs):
        @pl.when(exists(-k))
        def _():
            window(k, i).wait_recv()

    nkey = 4 + 3 * nv
    pairs = [(u, u + 6 + t) for u in range(nv) for t in range(-REACH, REACH + 1)]
    sc[...] = jnp.zeros_like(sc)

    def scores_of(s):
        qb[...] = dot_t(sw[6:6 + nv].reshape(rows, dm), wqs[s, :hw, :]).astype(BF16).reshape(nv, pp, hw)
        kvb[s] = dot_t(sw[1:1 + nkey].reshape(nkey * pp, dm), wqs[s, hw:, :]).astype(BF16).reshape(nkey, pp, 2 * hw)
        for i, (u, j) in enumerate(pairs):
            prod[i * pp:(i + 1) * pp, :] = (
                qb[u].astype(F32) * kvb[s, j - 1, :, :hw].astype(F32)
            ).astype(BF16)
        lane = lax.broadcasted_iota(jnp.int32, (hw, 128), 0) // HD + heads * s
        col = lax.broadcasted_iota(jnp.int32, (hw, 128), 1)
        sc[...] += dot(prod[...], (lane == col).astype(F32).astype(BF16))

    def soften():
        total = gids.shape[0]
        local_n = total // nv
        base = (var % local_n) * nv
        for u in range(nv):
            mine_group = gids[base + u]
            slabs = []
            for t in range(-REACH, REACH + 1):
                w = base + u + t
                inside = (w >= 0) & (w < total)
                at = jnp.minimum(jnp.maximum(w, 0), total - 1)
                i = pairs.index((u, u + 6 + t))
                ok = inside & (gids[at] == mine_group)
                slabs.append(jnp.where(ok, sc[i * pp:(i + 1) * pp, :] * HD ** (-0.5), -jnp.inf))
            top = functools.reduce(jnp.maximum, slabs)
            es = [jnp.exp(x - top) for x in slabs]
            den = functools.reduce(lambda a, b: a + b, es)
            for t, e in enumerate(es):
                i = u * (2 * REACH + 1) + t
                pb[i * pp:(i + 1) * pp, :] = (e / den).astype(BF16)

    def mix_of(s):
        lane = lax.broadcasted_iota(jnp.int32, (128, hw), 1) // HD + heads * s
        col = lax.broadcasted_iota(jnp.int32, (128, hw), 0)
        spread = (lane == col).astype(F32).astype(BF16)
        done = []
        for u in range(nv):
            total_u = jnp.zeros((pp, hw), F32)
            lo = u * (2 * REACH + 1)
            wide = dot(pb[lo * pp:(lo + 2 * REACH + 1) * pp, :], spread)
            for t in range(2 * REACH + 1):
                val = kvb[s, u + t, :, hw:].astype(F32)
                total_u = total_u + wide[t * pp:(t + 1) * pp] * val
            done.append(total_u.astype(BF16))
        res = dot(jnp.concatenate(done, axis=0), wos[s]).astype(BF16).astype(F32)
        return res

    scores_of(me)
    for d in (0, 1):
        wc[1, 4 + d].wait_recv()
        scores_of(side[d])
    w_diag(1)
    soften()
    mix2 = mix_of(me)
    for d in (0, 1):
        wc[2, 4 + d].wait_recv()
        mix2 = mix2 + mix_of(side[d])
    w_diag(2)
    wc[1, 6].wait_recv()
    scores_of(side[2])
    soften()
    wc[2, 6].wait_recv()
    mix2 = mix2 + mix_of(side[2])
    out[...] = (mid[...].astype(F32) + mix2).astype(BF16).reshape(nv, pp, dm)

    for c in sends:
        c.wait_send()
    for i, k in enumerate(nbrs):
        @pl.when(exists(k))
        def _():
            window(k, i).wait_send()


def on_device(n, nvar, tokens, patch_mask, group_ids, time_gain, time_qkv, time_out, space_gain, space_qkv, space_out):
    pp, nv, dm = tokens.shape
    hw = time_out.shape[0]
    tok = jnp.transpose(tokens, (1, 0, 2))
    wt = jnp.transpose(time_qkv, (1, 2, 0)).reshape(3 * hw, dm)
    wqs = jnp.transpose(space_qkv, (1, 2, 0)).reshape(3 * hw, dm)
    npair = nv * (2 * REACH + 1)
    vm = pl.BlockSpec(memory_space=pltpu.VMEM)
    anyv = pl.BlockSpec(memory_space=pltpu.HBM)
    dma = pltpu.SemaphoreType.DMA
    res = pl.pallas_call(
        functools.partial(kernel, n, nvar),
        out_shape=jax.ShapeDtypeStruct((nv, pp, dm), BF16),
        in_specs=[anyv, vm, pl.BlockSpec(memory_space=pltpu.SMEM), vm, vm, anyv, anyv, anyv, anyv],
        out_specs=vm,
        scratch_shapes=[
            pltpu.VMEM((nv, n * pp, dm), BF16),
            pltpu.VMEM((n, nv, pp), jnp.int32),
            pltpu.VMEM((3 * hw, dm), BF16),
            pltpu.VMEM((n, hw, dm), BF16),
            pltpu.VMEM((n, 3 * hw, dm), BF16),
            pltpu.VMEM((n, hw, dm), BF16),
            pltpu.VMEM((nv, n * pp, hw), BF16),
            pltpu.VMEM((n, nv, pp, hw), BF16),
            pltpu.VMEM((nv * pp, dm), BF16),
            pltpu.VMEM((5 * nv, pp, dm), BF16),
            pltpu.VMEM((n, 4 + 3 * nv, pp, 2 * hw), BF16),
            pltpu.VMEM((nv, pp, hw), BF16),
            pltpu.VMEM((npair * pp, hw), BF16),
            pltpu.VMEM((npair * pp, 128), F32),
            pltpu.VMEM((npair * pp, 128), BF16),
            dma((5,)), dma((3, 4)), dma((3, 4)), dma((3,)), dma((3,)),
            dma((3, 7)), dma((3, 7)), dma((nv, 3)), dma((nv, 3)), dma((4,)), dma((4,)),
        ],
        compiler_params=pltpu.CompilerParams(
            collective_id=0, has_side_effects=True, vmem_limit_bytes=67_000_000
        ),
    )(tok, patch_mask.T, group_ids, time_gain, space_gain, wt, time_out, wqs, space_out)
    return jnp.transpose(res, (1, 0, 2))


def solution(mesh):
    in_specs = (
        P("patch", ("parts", "var"), None),
        P("patch", ("parts", "var")),
        P("parts"),
        P(),
        P(None, None, "patch"),
        P("patch", None),
        P(),
        P(None, None, "patch"),
        P("patch", None),
    )
    out_specs = P("patch", ("parts", "var"), None)
    return jax.shard_map(
        functools.partial(on_device, mesh.shape["patch"], mesh.shape["var"]),
        mesh=mesh, in_specs=in_specs, out_specs=out_specs, check_vma=False,
    )
```

profile of v0, /device:TPU:0, one launch (start us, length us, event | category | flops | bytes accessed | tf_op | source)
XLA Modules:
  0.0 53.6 jit_solution(8685583336643167317)
XLA Ops:
  0.0 51.9 %shard_map.91 = bf16[3,64,768]{2,1,0:T(8,128)(2,1)} custom-call(bf16[3,64,768]{2,1,0:T(8,128)(2,1)} %bitcast.12, s32[3,64]{1,0:T(4,128)} %bitcast.13, s32[24]{0:T(128)} %gids.1, f32[768]{0:T(1024)} %tgain.1, f32[768]{0:T(1024)} %sgain.1, bf16[576,768]{1,0:T(8,128)(2,1)} %bitcast.10, bf16[192,768]{1,0:T(8,128)(2,1)} %wot_in.1, bf16[576,768]{1,0:T(8,128)(2,1)} %bitcast.11, ...), custom_call_target="tpu_custom_call" | custom-call | tf_op jit(solution)/shard_map/pallas_call | solution.py:304
  51.9 1.7 %copy.11 = bf16[64,3,768]{2,0,1:T(8,128)(2,1)} copy(bf16[64,3,768]{2,0,1:T(8,128)(2,1)} %bitcast.9) | data formatting | bytes 589824
where the time goes:
time: 53.8 us; the launch traced here: 53.6 us
  Pallas kernels  51.9 us (96%)
  local copies, waits for them, and re-layouts  1.69 us (3%)
    pallas_call x1, Pallas kernels, on_device(): pl.pallas_call(functools.partial(kernel, n, nvar), out_shape=jax.ShapeDty...  51.9 us
    unnamed x1, local copies, waits for them, and re-layouts  1.69 us

commit v1 on v0

--- a/solution.py
+++ b/solution.py
@@ -326,7 +326,7 @@
             dma((3, 7)), dma((3, 7)), dma((nv, 3)), dma((nv, 3)), dma((4,)), dma((4,)),
         ],
         compiler_params=pltpu.CompilerParams(
-            collective_id=0, has_side_effects=True, vmem_limit_bytes=67_000_000
+            collective_id=0, has_side_effects=True, vmem_limit_bytes=40_000_000
         ),
     )(tok, patch_mask.T, group_ids, time_gain, space_gain, wt, time_out, wqs, space_out)
     return jnp.transpose(res, (1, 0, 2))

time: 53.8 us -> 58.4 us (1.086)
  local copies, waits for them, and re-layouts: 1.69 us -> 7.32 us
  Pallas kernels: 51.9 us -> 50.7 us
    unnamed x1 -> x19, local copies, waits for them, and re-layouts: 1.69 us -> 7.32 us
    pallas_call x1, Pallas kernels: 51.9 us -> 50.7 us  [on_device(): pl.pallas_call(functools.partial(kernel, n, nvar), out_shape=jax.ShapeDty...]
where the time goes in v1:
time: 58.4 us; the launch traced here: 58.1 us
  Pallas kernels  50.7 us (87%)
  local copies, waits for them, and re-layouts  7.32 us (13%)
    pallas_call x1, Pallas kernels, on_device(): pl.pallas_call(functools.partial(kernel, n, nvar), out_shape=jax.ShapeDty...  50.7 us
    unnamed x19, local copies, waits for them, and re-layouts  7.32 us

profile of v1, /device:TPU:0, one launch (start us, length us, event | category | flops | bytes accessed | tf_op | source)
XLA Modules:
  0.0 58.1 jit_solution(7006427821301363929)
XLA Ops:
  0.0 0.0 copy-start.5
  0.0 0.0 copy-start.7
  0.0 0.0 copy-start.8
  0.0 0.7 %copy-done.5 = f32[768]{0:T(1024)S(1)} copy-done((f32[768]{0:T(1024)S(1)}, f32[768]{0:T(1024)}, u32[]{:S(2)}) %copy-start.5) | copy-done | bytes 3096
  0.7 0.0 copy-done.7
  0.7 0.0 copy-done.8
  0.7 0.0 copy-start
  0.7 1.2 %copy-done = bf16[768,3,192]{0,2,1:T(8,128)(2,1)S(1)} copy-done((bf16[768,3,192]{0,2,1:T(8,128)(2,1)S(1)}, bf16[768,3,192]{0,2,1:T(8,128)(2,1)}, u32[]{:S(2)}) %copy-start) | copy-done | bytes 884760
  1.9 0.0 copy-start.1
  1.9 1.2 %copy-done.1 = bf16[768,3,192]{0,2,1:T(8,128)(2,1)S(1)} copy-done((bf16[768,3,192]{0,2,1:T(8,128)(2,1)S(1)}, bf16[768,3,192]{0,2,1:T(8,128)(2,1)}, u32[]{:S(2)}) %copy-start.1) | copy-done | bytes 884760
  3.0 0.0 copy-start.2
  3.0 1.0 %copy-done.2 = bf16[64,3,768]{2,0,1:T(8,128)(2,1)S(1)} copy-done((bf16[64,3,768]{2,0,1:T(8,128)(2,1)S(1)}, bf16[64,3,768]{2,0,1:T(8,128)(2,1)}, u32[]{:S(2)}) %copy-start.2) | copy-done | bytes 294936
  4.0 0.0 copy-start.3
  4.0 1.0 %copy-done.3 = bf16[192,768]{1,0:T(8,128)(2,1)S(1)} copy-done((bf16[192,768]{1,0:T(8,128)(2,1)S(1)}, bf16[192,768]{1,0:T(8,128)(2,1)}, u32[]{:S(2)}) %copy-start.3) | copy-done | bytes 294936
  5.0 0.0 copy-start.4
  5.0 1.0 %copy-done.4 = bf16[192,768]{1,0:T(8,128)(2,1)S(1)} copy-done((bf16[192,768]{1,0:T(8,128)(2,1)S(1)}, bf16[192,768]{1,0:T(8,128)(2,1)}, u32[]{:S(2)}) %copy-start.4) | copy-done | bytes 294936
  5.9 0.0 copy-start.6
  5.9 0.7 %copy-done.6 = f32[768]{0:T(1024)S(1)} copy-done((f32[768]{0:T(1024)S(1)}, f32[768]{0:T(1024)}, u32[]{:S(2)}) %copy-start.6) | copy-done | bytes 3096
  6.6 50.7 %shard_map.91 = bf16[3,64,768]{2,1,0:T(8,128)(2,1)S(1)} custom-call(bf16[3,64,768]{2,1,0:T(8,128)(2,1)S(1)} %bitcast.12, s32[3,64]{1,0:T(4,128)S(1)} %bitcast.13, s32[24]{0:T(128)S(1)} %copy-done.8, f32[768]{0:T(1024)S(1)} %copy-done.5, f32[768]{0:T(1024)S(1)} %copy-done.6, bf16[576,768]{1,0:T(8,128)(2,1)S(1)} %bitcast.10, bf16[192,768]{1,0:T(8,128)(2,1)S(1)} %copy-done.3, ...), custom_call_target="tpu_custom_call" | custom-call | tf_op jit(solution)/shard_map/pallas_call | solution.py:304
  57.3 0.7 %copy.11 = bf16[64,3,768]{2,0,1:T(8,128)(2,1)} copy(bf16[64,3,768]{2,0,1:T(8,128)(2,1)S(1)} %bitcast.9) | data formatting | bytes 589824
Async XLA Ops:
  0.0 0.7 %copy-start.5 = (f32[768]{0:T(1024)S(1)}, f32[768]{0:T(1024)}, u32[]{:S(2)}) copy-start(f32[768]{0:T(1024)} %tgain.1) | copy-start | bytes 9220
  0.0 0.7 %copy-start.7 = (s32[64,3]{0,1:T(4,128)S(1)}, s32[64,3]{0,1:T(4,128)}, u32[]{:S(2)}) copy-start(s32[64,3]{0,1:T(4,128)} %param.10) | copy-start | bytes 2308
  0.0 0.7 %copy-start.8 = (s32[24]{0:T(128)S(1)}, s32[24]{0:T(128)}, u32[]{:S(2)}) copy-start(s32[24]{0:T(128)} %gids.1) | copy-start | bytes 292
  0.7 1.2 %copy-start = (bf16[768,3,192]{0,2,1:T(8,128)(2,1)S(1)}, bf16[768,3,192]{0,2,1:T(8,128)(2,1)}, u32[]{:S(2)}) copy-start(bf16[768,3,192]{0,2,1:T(8,128)(2,1)} %param.13) | copy-start | bytes 2654212
  1.9 1.2 %copy-start.1 = (bf16[768,3,192]{0,2,1:T(8,128)(2,1)S(1)}, bf16[768,3,192]{0,2,1:T(8,128)(2,1)}, u32[]{:S(2)}) copy-start(bf16[768,3,192]{0,2,1:T(8,128)(2,1)} %param.16) | copy-start | bytes 2654212
  3.0 1.0 %copy-start.2 = (bf16[64,3,768]{2,0,1:T(8,128)(2,1)S(1)}, bf16[64,3,768]{2,0,1:T(8,128)(2,1)}, u32[]{:S(2)}) copy-start(bf16[64,3,768]{2,0,1:T(8,128)(2,1)} %param.9) | copy-start | bytes 884740
  4.0 1.0 %copy-start.3 = (bf16[192,768]{1,0:T(8,128)(2,1)S(1)}, bf16[192,768]{1,0:T(8,128)(2,1)}, u32[]{:S(2)}) copy-start(bf16[192,768]{1,0:T(8,128)(2,1)} %wot_in.1) | copy-start | bytes 884740
  5.0 1.0 %copy-start.4 = (bf16[192,768]{1,0:T(8,128)(2,1)S(1)}, bf16[192,768]{1,0:T(8,128)(2,1)}, u32[]{:S(2)}) copy-start(bf16[192,768]{1,0:T(8,128)(2,1)} %wos_in.1) | copy-start | bytes 884740
  5.9 0.7 %copy-start.6 = (f32[768]{0:T(1024)S(1)}, f32[768]{0:T(1024)}, u32[]{:S(2)}) copy-start(f32[768]{0:T(1024)} %sgain.1) | copy-start | bytes 9220

commit v2 on v1

v2 whole, which is shorter than its diff:
```python
import functools

import jax
import jax.numpy as jnp
from jax import lax
from jax.experimental import pallas as pl
from jax.experimental.pallas import tpu as pltpu
from jax.sharding import PartitionSpec as P

HD = 64
REACH = 5
TILE = 16
KEYS = 256
BATCH = 6
EPS = 1e-06
MESH = pl.DeviceIdType.MESH
F32 = jnp.float32
BF16 = jnp.bfloat16

GROUPS = ("q", "k", "v", "ot", "os")
SHARED = ('ot', 'k', 'v')
SPLIT = ()
PLAN = (
    "ot:D", "k:D", "n", "init", "v:D", "t0", "ot:Z", "t2", "v:R", "t1", "v:Z", "tr0",
    "k:Z", "ot:R", "tr2", "v:G", "tr1", "k:R", "c0", "ot:G", "c2", "c1", "q:D", "ot:T",
    "k:G", "ot:U", "m0", "os:D", "k:T", "k:U", "m2", "v:T", "v:U", "m1", "Ak", "Av",
    "q:R", "os:R", "Hk", "Hv", "q:G", "Aq", "S0", "os:G", "S1", "O",
)


def norm_rows(rows, gain):
    floats = rows.astype(F32)
    scaled = floats * lax.rsqrt(jnp.mean(floats * floats, axis=-1, keepdims=True) + EPS)
    return (scaled * gain).astype(BF16)


def dot(a, b):
    return jnp.dot(a, b, preferred_element_type=F32)


def dot_t(a, b):
    return lax.dot_general(a, b, (((1,), (1,)), ((), ())), preferred_element_type=F32)


def sem_names(nv):
    names = ["mk", "near", "far"]
    for v in range(nv):
        names += [("t", v), ("tr", v), ("a", v)]
    for g in GROUPS:
        names += [("w", g), ("wr", g), ("ws", g, 0), ("ws", g, 1)]
        if g in SHARED:
            names += [("wz", g, 0), ("wt", g, 0)]
        if g in SHARED + SPLIT:
            names += [("wz", g, 1), ("wt", g, 1)]
    return {name: i for i, name in enumerate(names + [(w, g) for w in ("ko", "kh") for g in "kv"])}


def kernel(
    n, nvar, tok, marks, gids_in, tgain_in, sgain_in, wt_in, wot_in, wqs_in, wos_in,
    out, gx, raw, mk, wt, wall, att, att_b, ratt, ratt_b, mid, sx, kv, qb, mask, att2,
    gids, tgain, sgain, local_sem, recv, send,
):
    me = lax.axis_index("patch")
    var = lax.axis_index("var")
    nv, pp, dm = tok.shape
    hw = wot_in.shape[0]
    heads = hw // HD
    full = n * pp
    rows = nv * pp
    wide = 2 * HD
    slots = 2 * REACH + nv
    side = (me + 1 - 2 * (me % 2), me + 2 - 4 * ((me // 2) % 2), n - 1 - me)
    order = (me, side[0], side[1], side[2])
    core = var % 2
    sib = var + 1 - 2 * core
    plane = (var // 2) % 2
    mate = var + 2 - 4 * plane
    near = var + 2 * core - 1
    far = var + 2 - 4 * core
    near_ok = (near >= 0) & (near < nvar)
    far_ok = (far >= 0) & (far < nvar)
    own0 = (1 - core) * REACH
    out0 = core * nv
    names = sem_names(nv)

    barrier = pltpu.get_barrier_semaphore()
    count = n - 1
    for other in side:
        pl.semaphore_signal(barrier, inc=1, device_id={"patch": other}, device_id_type=MESH)
    for k in (1, -1, 2, -2):
        there = (var + k >= 0) & (var + k < nvar)

        @pl.when(there)
        def _():
            pl.semaphore_signal(barrier, inc=1, device_id={"var": var + k}, device_id_type=MESH)
        count = count + there.astype(jnp.int32)

    def base(g, shard):
        return (GROUPS.index(g) * n + shard) * hw

    def wrows(g, shard, lo, num, cols=None):
        at = pl.ds(pl.multiple_of(base(g, shard) + lo, 16), num)
        return wall.at[at, :] if cols is None else wall.at[at, pl.ds(cols * (dm // 2), dm // 2)]

    def source(g, lo, num):
        if g == "ot":
            return wot_in.at[pl.ds(pl.multiple_of(lo, 16), num), :]
        if g == "os":
            return wos_in.at[pl.ds(pl.multiple_of(lo, 16), num), :]
        return wqs_in.at[pl.ds(pl.multiple_of(("q", "k", "v").index(g) * hw + lo, 16), num), :]

    def mine(g):
        num = hw // 4 if g in SHARED else hw // 2
        return (2 * plane + core if g in SHARED else core) * num, num

    def part(g, other=0):
        if g not in SHARED + SPLIT:
            return mine(g)
        num = hw // 4
        which = plane if other == 0 else 1 - plane
        return (2 * which + core if g in SHARED else 2 * core + which) * num, num

    def mine_rows(g):
        return wall.at[pl.ds(pl.multiple_of(base(g, me), hw), hw), :]

    own = [
        pltpu.make_async_copy(tok, raw, local_sem.at[0]),
        pltpu.make_async_copy(wt_in, wt, local_sem.at[1]),
    ] + [
        pltpu.make_async_copy(source(g, 0, hw), mine_rows(g), local_sem.at[2 + i]) for i, g in enumerate(GROUPS)
    ] + [
        pltpu.make_async_copy(a, b, local_sem.at[2 + len(GROUPS) + i])
        for i, (a, b) in enumerate(((tgain_in, tgain), (sgain_in, sgain), (gids_in, gids), (marks, mk.at[me])))
    ]
    for i in (0, 2 + len(GROUPS), *range(1, 2 + len(GROUPS)), *range(3 + len(GROUPS), len(own))):
        own[i].start()
    pl.semaphore_wait(barrier, count)

    sent = {"w": 0, "x": 0}
    waited = set()

    def push(kind, src, dst, name, size, **where):
        lane = ("w", "x", "mk", "near", "far").index(kind)
        if kind in sent:
            sent[kind] += size
        pltpu.make_async_remote_copy(
            src_ref=src, dst_ref=dst, send_sem=send.at[lane], recv_sem=recv.at[names[name]],
            device_id=where, device_id_type=MESH,
        ).start()

    def drain(sem, num):
        settle(sem, wall.at[pl.ds(0, num), :])

    def settle(sem, ref):
        pltpu.make_async_copy(ref, ref, sem).wait()

    def need(name, num, ref=None):
        if name not in waited:
            waited.add(name)
            settle(recv.at[names[name]], wall.at[pl.ds(0, num), :] if ref is None else ref)

    def need_own(i):
        if ("own", i) not in waited:
            waited.add(("own", i))
            own[i].wait()

    def block(of, lo=0, num=pp):
        return pl.ds(pl.multiple_of(of * pp + lo, num), num)

    half = pp // 2

    def tokens(v):
        for d in (0, 1):
            piece = gx.at[v, block(me), :]
            push("x", piece, piece, ("t", v), pp, patch=side[d])

    def tokens_relay(v):
        need(("t", v), 2 * pp)
        for d in (0, 1):
            piece = gx.at[v, block(side[1 - d], d * half, half), :]
            push("x", piece, piece, ("tr", v), half, patch=side[d])

    def w_direct(g):
        lo, num = mine(g)
        for d in (0, 1):
            push("w", source(g, lo, num), wrows(g, me, lo, num), ("w", g), num, patch=side[d])

    def w_relay(g):
        lo, num = mine(g)
        need(("w", g), 2 * num)
        low, few = part(g)
        for d in (0, 1):
            piece = wrows(g, side[1 - d], low, few, d)
            push("w", piece, piece, ("wr", g), few // 2, patch=side[d])
        for d in (0, 1):
            piece = wrows(g, side[d], lo, num)
            push("w", piece, piece, ("ws", g, 0), num, var=sib)

    def w_mate(g):
        lo, num = mine(g)
        need(("w", g), 2 * num)
        for d in (0, 1):
            piece = wrows(g, side[d], lo, num)
            push("w", piece, piece, ("wz", g, 0), num, var=mate)

    def w_diag(g):
        lo, num = part(g)
        need(("wr", g), num)
        piece = wrows(g, side[2], lo, num)
        push("w", piece, piece, ("ws", g, 1), num, var=sib)
        if g in SHARED + SPLIT:
            push("w", piece, piece, ("wz", g, 1), num, var=mate)

    def w_share(g, j):
        lo, num = part(g, 1)
        need(("wz", g, j), (2 - j) * num)
        for d in ((0, 1), (2,))[j]:
            piece = wrows(g, side[d], lo, num)
            push("w", piece, piece, ("wt", g, j), num, var=sib)

    def have(g, j):
        if j == 0:
            need_own(2 + GROUPS.index(g))
            return
        i = j // 3
        num = (part(g) if i else mine(g))[1]
        need(("ws", g, i), (2 - i) * num)
        if g in SHARED or (i and g in SPLIT):
            need(("wt", g, i), (2 - i) * num)

    def init():
        need_own(4 + len(GROUPS))
        total = gids.shape[0]
        start = (var % (total // nv)) * nv
        slot = lax.broadcasted_iota(jnp.int32, (TILE, KEYS), 1) // TILE
        same = lax.broadcasted_iota(jnp.int32, (TILE, KEYS), 0) == lax.broadcasted_iota(jnp.int32, (TILE, KEYS), 1) % TILE
        for u in range(nv):
            mine_group = gids[start + u]
            line = jnp.full((TILE, KEYS), -jnp.inf, F32)
            for i in range(slots):
                w = start + i - REACH
                inside = (w >= 0) & (w < total)
                at = jnp.minimum(jnp.maximum(w, 0), total - 1)
                ok = jnp.where(inside & (gids[at] == mine_group), 0.0, -jnp.inf).astype(F32)
                line = jnp.where(slot == i, ok, line)
            mask[u * TILE:(u + 1) * TILE] = jnp.where(same, line, -jnp.inf)

        @pl.when(jnp.logical_not(near_ok))
        def _():
            sx[pl.ds(out0, REACH)] = jnp.zeros((REACH, pp, dm), BF16)

    def normalize():
        need_own(0)
        need_own(2 + len(GROUPS))
        for v in range(nv):
            gx[v, block(me), :] = norm_rows(raw[v], tgain[...])

    lane_h = lax.broadcasted_iota(jnp.int32, (1, hw), 1) // HD
    blk = full // 2

    def time_of(v):
        need(("tr", v), pp)
        need_own(1)
        need("mk", 0, mk.at[pl.ds(0, n - 1)])
        need_own(5 + len(GROUPS))
        seen = jnp.concatenate([mk[s][v:v + 1] for s in range(n)], axis=1)
        normed = gx[v]
        q = dot_t(normed, wt[0:hw, :]).astype(BF16)
        k = dot_t(normed, wt[hw:2 * hw, :]).astype(BF16)
        val = dot_t(normed, wt[2 * hw:3 * hw, :]).astype(BF16)
        qs = [q * jnp.where(lane_h == h, HD ** (-0.5), 0.0).astype(BF16) for h in range(heads)]
        todo = [(b, h) for b in range(2) for h in range(heads)]
        allowed = []
        for b in range(2):
            keys = (b + 1) * blk
            qi = lax.broadcasted_iota(jnp.int32, (blk, keys), 0) + b * blk
            ki = lax.broadcasted_iota(jnp.int32, (blk, keys), 1)
            allowed.append(((ki < qi) & (seen[:, :keys] > 0)) | (ki == qi))
        ss = [dot_t(qs[h][b * blk:(b + 1) * blk], k[:(b + 1) * blk]) for b, h in todo]
        ss = [jnp.where(allowed[b], s, -jnp.inf) for (b, h), s in zip(todo, ss)]
        tops = [jnp.max(s, axis=-1, keepdims=True) for s in ss]
        es = [jnp.exp(s - m) for s, m in zip(ss, tops)]
        dens = [1.0 / jnp.sum(e, axis=-1, keepdims=True) for e in es]
        ws = [(e * d).astype(BF16) for e, d in zip(es, dens)]
        os = [dot(w, val[:(b + 1) * blk]) for (b, h), w in zip(todo, ws)]
        for b in range(2):
            res = os[b * heads]
            for h in range(1, heads):
                res = jnp.where(lane_h == h, os[b * heads + h], res)
            att[v, b * blk:(b + 1) * blk, :] = res[:, :wide].astype(BF16)
            tail = res[:, wide:]
            for i in range(blk // pp):
                lo = b * blk + i * pp
                pair = jnp.concatenate([tail[i * pp:i * pp + half], tail[i * pp + half:(i + 1) * pp]], axis=1)
                att_b[v, lo // 2:lo // 2 + half, :] = pair.astype(BF16)
        for d in (2, 0, 1):
            push("x", att.at[v, block(side[d]), :], ratt.at[me, v], ("a", v), pp * hw // dm, patch=side[d])
            at = pl.ds(pl.multiple_of(side[d] * half, half), half)
            push("x", att_b.at[v, at, :], ratt_b.at[me, v], ("a", v), 0, patch=side[d])
        ratt[me, v] = att[v, block(me), :]
        ratt_b[me, v] = att_b[v, pl.ds(pl.multiple_of(me * half, half), half), :]

    def middle_of(v):
        need(("a", v), (n - 1) * pp * hw // dm)
        for j in (0, 1, 3):
            have("ot", j)
        mix = jnp.zeros((pp, dm), F32)
        for s in range(n):
            pair = ratt_b[s, v]
            tail = jnp.concatenate([pair[:, :hw - wide], pair[:, hw - wide:]], axis=0)
            mix = mix + dot(jnp.concatenate([ratt[s, v], tail], axis=1), wall[base("ot", s):base("ot", s) + hw, :])
        need_own(3 + len(GROUPS))
        middle = (raw[v].astype(F32) + mix).astype(BF16)
        mid[v * pp:(v + 1) * pp, :] = middle
        sx[own0 + v] = norm_rows(middle, sgain[...])

        @pl.when(near_ok)
        def _():
            push("near", sx.at[own0 + v], sx.at[3 - core + v], "near", pp, var=near)

        @pl.when(far_ok & (v - 1 + core >= 0) & (v - 1 + core < 2))
        def _():
            push("far", sx.at[own0 + v], sx.at[7 * core + v - 1], "far", pp, var=far)

    def halo():
        if "halo" in waited:
            return
        waited.add("halo")

        @pl.when(near_ok)
        def _():
            drain(recv.at[names["near"]], nv * pp)
            drain(recv.at[names["far"]], 2 * pp)

    def weight(g):
        for j in (0, 1, 3):
            have(g, j)
        return wall[base(g, 0):base(g, n), :]

    def pass_on(g, name, src, dst, num):
        t = "kv".index(g)
        push("x", kv.at[t, pl.ds(src, num)], kv.at[t, pl.ds(dst, num)], (name, g), num * pp, var=sib)

    def own_part(g):
        x = sx[pl.ds(own0, nv)].reshape(rows, dm)
        part = dot_t(x, weight(g)).astype(BF16)
        if g == "q":
            qb[...] = part * jnp.asarray(HD ** (-0.5), BF16)
        else:
            kv["kv".index(g), REACH:REACH + nv] = part.reshape(nv, pp, dm)
            pass_on(g, "ko", REACH, REACH - nv + 2 * nv * core, nv)

    def halo_part(g):
        halo()
        x = sx[pl.ds(out0, REACH)].reshape(REACH * pp, dm)
        part = dot_t(x, weight(g)).astype(BF16)
        kv["kv".index(g), pl.ds(core * (REACH + nv), REACH)] = part.reshape(REACH, pp, dm)
        pass_on(g, "kh", REACH - 2 + (nv + 2) * core, (REACH + 2 * nv) * core, REACH - nv)

    lane_k = lax.broadcasted_iota(jnp.int32, (1, KEYS), 1) // HD
    pack = KEYS // HD

    def space(which):
        for g in "kv":
            need(("ko", g), nv * pp)
            need(("kh", g), (REACH - nv) * pp)
        bias = jnp.concatenate([mask[...]] * pack, axis=0)
        blank = jnp.zeros((KEYS - slots * TILE, KEYS), BF16)
        num = nv * TILE
        todo = [(b, c) for b in range(2 * which, 2 * which + 2) for c in range(dm // KEYS)]

        def picks(t, b, on):
            at = slice(b * TILE, (b + 1) * TILE)
            return jnp.concatenate([kv[t, i, at, on] for i in range(slots)] + [blank], axis=0)

        for lo in range(0, len(todo), BATCH):
            part = todo[lo:lo + BATCH]
            ss = []
            for b, c in part:
                on = slice(c * KEYS, (c + 1) * KEYS)
                q = jnp.concatenate([qb[u * pp + b * TILE:u * pp + (b + 1) * TILE, on] for u in range(nv)], axis=0)
                many = jnp.concatenate([q * (lane_k == h).astype(F32).astype(BF16) for h in range(pack)], axis=0)
                ss.append(dot_t(many, picks(0, b, on)) + bias)
            tops = [jnp.max(s, axis=-1, keepdims=True) for s in ss]
            es = [jnp.exp(s - m) for s, m in zip(ss, tops)]
            dens = [1.0 / jnp.sum(e, axis=-1, keepdims=True) for e in es]
            ws = [(e * d).astype(BF16) for e, d in zip(es, dens)]
            for (b, c), w in zip(part, ws):
                on = slice(c * KEYS, (c + 1) * KEYS)
                o = dot(w, picks(1, b, on))
                res = o[:num]
                for h in range(1, pack):
                    res = jnp.where(lane_k == h, o[h * num:(h + 1) * num], res)
                res = res.astype(BF16)
                for u in range(nv):
                    att2[u * pp + b * TILE:u * pp + (b + 1) * TILE, on] = res[u * TILE:(u + 1) * TILE]

    def finish():
        total = mid[...].astype(F32) + dot(att2[...], weight("os"))
        out[...] = total.astype(BF16).reshape(nv, pp, dm)

    for d in range(3):
        push("mk", marks, mk.at[me], "mk", 0, patch=side[d])
    steps = {"D": w_direct, "R": w_relay, "Z": w_mate, "G": w_diag}
    calls = {"t": tokens, "tr": tokens_relay, "c": time_of, "m": middle_of, "S": space}
    parts = {"A": own_part, "H": halo_part}
    once = {"init": init, "n": normalize, "O": finish}
    for step in PLAN:
        if step in once:
            once[step]()
        elif step[0] in parts:
            parts[step[0]](step[1])
        elif ":" in step:
            g, what = step.split(":")
            if what in steps:
                steps[what](g)
            else:
                w_share(g, "TU".index(what))
        else:
            calls[step[:-1]](int(step[-1]))

    for i in range(len(own)):
        need_own(i)
    drain(send.at[0], sent["w"])
    drain(send.at[1], sent["x"])
    settle(send.at[2], mk.at[pl.ds(0, n - 1)])

    @pl.when(near_ok)
    def _():
        drain(send.at[3], nv * pp)

    @pl.when(far_ok)
    def _():
        drain(send.at[4], 2 * pp)


def on_device(n, nvar, tokens, patch_mask, group_ids, time_gain, time_qkv, time_out, space_gain, space_qkv, space_out):
    pp, nv, dm = tokens.shape
    hw = time_out.shape[0]
    tok = jnp.transpose(tokens, (1, 0, 2))
    wt = jnp.transpose(time_qkv, (1, 2, 0)).reshape(3 * hw, dm)
    wqs = jnp.transpose(space_qkv, (1, 2, 0)).reshape(3 * hw, dm)
    vm = pl.BlockSpec(memory_space=pltpu.VMEM)
    anyv = pl.BlockSpec(memory_space=pltpu.HBM)
    dma = pltpu.SemaphoreType.DMA
    res = pl.pallas_call(
        functools.partial(kernel, n, nvar),
        out_shape=jax.ShapeDtypeStruct((nv, pp, dm), BF16),
        in_specs=[anyv] * 9,
        out_specs=vm,
        scratch_shapes=[
            pltpu.VMEM((nv, n * pp, dm), BF16),
            pltpu.VMEM((nv, pp, dm), BF16),
            pltpu.VMEM((n, nv, pp), jnp.int32),
            pltpu.VMEM((3 * hw, dm), BF16),
            pltpu.VMEM((5 * n * hw, dm), BF16),
            pltpu.VMEM((nv, n * pp, 2 * HD), BF16),
            pltpu.VMEM((nv, n * pp // 2, 2 * HD), BF16),
            pltpu.VMEM((n, nv, pp, 2 * HD), BF16),
            pltpu.VMEM((n, nv, pp // 2, 2 * HD), BF16),
            pltpu.VMEM((nv * pp, dm), BF16),
            pltpu.VMEM((REACH + nv, pp, dm), BF16),
            pltpu.VMEM((2, 2 * REACH + nv, pp, dm), BF16),
            pltpu.VMEM((nv * pp, dm), BF16),
            pltpu.VMEM((nv * TILE, KEYS), F32),
            pltpu.VMEM((nv * pp, dm), BF16),
            pltpu.SMEM(group_ids.shape, jnp.int32),
            pltpu.VMEM((dm,), F32),
            pltpu.VMEM((dm,), F32),
            dma((6 + len(GROUPS),)), dma((len(sem_names(nv)),)), dma((5,)),
        ],
        compiler_params=pltpu.CompilerParams(
            collective_id=0, has_side_effects=True, vmem_limit_bytes=56_200_000
        ),
    )(tok, patch_mask.T, group_ids, time_gain, space_gain, wt, time_out, wqs, space_out)
    return jnp.transpose(res, (1, 0, 2))


def solution(mesh):
    in_specs = (
        P("patch", ("parts", "var"), None),
        P("patch", ("parts", "var")),
        P("parts"),
        P(),
        P(None, None, "patch"),
        P("patch", None),
        P(),
        P(None, None, "patch"),
        P("patch", None),
    )
    out_specs = P("patch", ("parts", "var"), None)
    return jax.shard_map(
        functools.partial(on_device, mesh.shape["patch"], mesh.shape["var"]),
        mesh=mesh, in_specs=in_specs, out_specs=out_specs, check_vma=False,
    )
```

time: 58.4 us -> 41.6 us (0.71)
  Pallas kernels: 50.7 us -> 39.2 us
  local copies, waits for them, and re-layouts: 7.32 us -> 2.1 us
    pallas_call x1, Pallas kernels: 50.7 us -> 39.2 us  [on_device(): pl.pallas_call(functools.partial(kernel, n, nvar), out_shape=jax.ShapeDty...]
    unnamed x19 -> x9, local copies, waits for them, and re-layouts: 7.32 us -> 2.1 us
where the time goes in v2:
time: 41.6 us; the launch traced here: 41.3 us
  Pallas kernels  39.2 us (94%)
  local copies, waits for them, and re-layouts  2.1 us (5%)
    pallas_call x1, Pallas kernels, on_device(): pl.pallas_call(functools.partial(kernel, n, nvar), out_shape=jax.ShapeDty...  39.2 us
    unnamed x9, local copies, waits for them, and re-layouts  2.1 us

profile of v2, /device:TPU:0, one launch (start us, length us, event | category | flops | bytes accessed | tf_op | source)
XLA Modules:
  0.0 41.3 jit_solution(78951800504549237)
XLA Ops:
  0.0 0.0 copy-start
  0.0 0.0 copy-start.2
  0.0 0.0 copy-start.3
  0.0 0.7 %copy-done = f32[768]{0:T(1024)S(1)} copy-done((f32[768]{0:T(1024)S(1)}, f32[768]{0:T(1024)}, u32[]{:S(2)}) %copy-start) | copy-done | bytes 3096
  0.7 0.0 copy-done.2
  0.7 0.0 copy-done.3
  0.7 0.0 copy-start.1
  0.7 0.7 %copy-done.1 = f32[768]{0:T(1024)S(1)} copy-done((f32[768]{0:T(1024)S(1)}, f32[768]{0:T(1024)}, u32[]{:S(2)}) %copy-start.1) | copy-done | bytes 3096
  1.4 39.2 %shard_map.91 = bf16[3,64,768]{2,1,0:T(8,128)(2,1)S(1)} custom-call(bf16[3,64,768]{2,1,0:T(8,128)(2,1)} %bitcast.13, s32[3,64]{1,0:T(4,128)S(1)} %bitcast.10, s32[24]{0:T(128)S(1)} %copy-done.3, f32[768]{0:T(1024)S(1)} %copy-done, f32[768]{0:T(1024)S(1)} %copy-done.1, bf16[576,768]{1,0:T(8,128)(2,1)} %bitcast.11, bf16[192,768]{1,0:T(8,128)(2,1)} %wot_in.1, ...), custom_call_target="tpu_custom_call" | custom-call | tf_op jit(solution)/shard_map/pallas_call | solution.py:446
  40.6 0.7 %copy.11 = bf16[64,3,768]{2,0,1:T(8,128)(2,1)} copy(bf16[64,3,768]{2,0,1:T(8,128)(2,1)S(1)} %bitcast.9) | data formatting | bytes 589824
Async XLA Ops:
  0.0 0.7 %copy-start = (f32[768]{0:T(1024)S(1)}, f32[768]{0:T(1024)}, u32[]{:S(2)}) copy-start(f32[768]{0:T(1024)} %tgain_in.1) | copy-start | bytes 9220
  0.0 0.7 %copy-start.2 = (s32[64,3]{0,1:T(4,128)S(1)}, s32[64,3]{0,1:T(4,128)}, u32[]{:S(2)}) copy-start(s32[64,3]{0,1:T(4,128)} %param.10) | copy-start | bytes 2308
  0.0 0.7 %copy-start.3 = (s32[24]{0:T(128)S(1)}, s32[24]{0:T(128)}, u32[]{:S(2)}) copy-start(s32[24]{0:T(128)} %gids_in.1) | copy-start | bytes 292
  0.7 0.7 %copy-start.1 = (f32[768]{0:T(1024)S(1)}, f32[768]{0:T(1024)}, u32[]{:S(2)}) copy-start(f32[768]{0:T(1024)} %sgain_in.1) | copy-start | bytes 9220
